TPU v7x, 32 devices: a whole 2x2x4 slice. The times are simulated.
32 devices in a mesh: pop: 16 (over z, y, core), shard: 2 (over x).
Axes of the slice: x: 2, y: 2, z: 4, core: 2. Of those that a mesh axis runs over, the one named last changes fastest.
Arguments:
- hidden: bfloat16 [2048, 4096], P('pop'), may hold values from -6 to 6
- weight: bfloat16 [4096, 14336], P('pop', 'shard'), may hold values from -0.09375 to 0.09375
- left_factors: bfloat16 [128, 4096], P('pop'), may hold values from -6 to 6
- right_factors: bfloat16 [128, 14336], P('pop', 'shard'), may hold values from -6 to 6
- target: bfloat16 [2048, 14336], P('pop', 'shard'), may hold values from -6 to 6
Outputs:
- up_out: bfloat16 [2048, 14336], P('pop', 'shard')
- step: float32 [4096, 14336], P('pop', 'shard')
- fitness: float32 [128], P('pop')
All inputs are finite; a program needn't handle non-finite values.
Results may differ from a plain program's by a relative error of at most 0.001.
Values may be sent and summed in bfloat16 or wider, within the bound.
A program may use at most 128 MiB of HBM per device.

v0:
```python
import math

import jax
import jax.numpy as jnp
from jax import lax
from jax.sharding import PartitionSpec as P

noise_scale = 0.5
spread_eps = 1e-05


def split_parts(values):
    high = values.astype(jnp.bfloat16)
    kept = lax.optimization_barrier(high)
    low = (values - kept.astype(jnp.float32)).astype(jnp.bfloat16)
    return (high, low)


def local(hidden, weight, left_factors, right_factors, target):
    local_members = left_factors.shape[0]
    row_count = hidden.shape[0]
    token_count = row_count // local_members
    feature_count = hidden.shape[1]
    local_cols = weight.shape[1]
    member_count = local_members * lax.axis_size("pop")
    base_out = jnp.dot(
        hidden,
        lax.all_gather(weight, "pop", axis=0, tiled=True),
        preferred_element_type=jnp.float32,
    )
    grouped = hidden.reshape(local_members, token_count, feature_count)
    projected = jnp.einsum(
        "mtd,md->mt", grouped, left_factors, preferred_element_type=jnp.float32
    ) / math.sqrt(feature_count)
    right_wide = right_factors.astype(jnp.float32)
    perturbed = (
        base_out.reshape(local_members, token_count, local_cols)
        + noise_scale * projected[:, :, None] * right_wide[:, None, :]
    )
    up_out = perturbed.astype(jnp.bfloat16).reshape(row_count, local_cols)
    directions = target.reshape(local_members, token_count, local_cols).astype(jnp.float32)
    partial_value = jnp.sum(jax.nn.silu(perturbed) * directions, axis=(1, 2))
    reward = lax.psum(partial_value, "shard")
    first_sum, second_sum = lax.psum((jnp.sum(reward), jnp.sum(reward * reward)), "pop")
    mean_reward = first_sum / member_count
    spread = second_sum / member_count - mean_reward * mean_reward
    fitness = (reward - mean_reward) / jnp.sqrt(spread + spread_eps)
    weighted = left_factors.astype(jnp.float32) * fitness[:, None]
    weighted_all = lax.all_to_all(weighted, "pop", split_axis=1, concat_axis=0, tiled=True)
    weighted_high, weighted_low = split_parts(weighted_all)
    contract = (((0,), (0,)), ((), ()))
    portion = lax.all_gather(right_factors, "pop", axis=0, tiled=True)
    upper = lax.dot_general(weighted_high, portion, contract, preferred_element_type=jnp.float32)
    lower = lax.dot_general(weighted_low, portion, contract, preferred_element_type=jnp.float32)
    summed = upper + lower
    step = summed / math.sqrt(member_count)
    return (up_out, step, fitness)


def solution(mesh):
    in_specs = (
        P("pop", None),
        P("pop", "shard"),
        P("pop", None),
        P("pop", "shard"),
        P("pop", "shard"),
    )
    out_specs = (P("pop", "shard"), P("pop", "shard"), P("pop"))
    return jax.shard_map(local, mesh=mesh, in_specs=in_specs, out_specs=out_specs, check_vma=False)
```

profile of v0, /device:TPU:0, one launch (start us, length us, event | category | flops | bytes accessed | tf_op | source)
XLA Modules:
  0.0 387.5 jit_solution(8941407675509226462)
XLA Ops:
  7.2 0.0 copy-start
  7.2 0.0 copy-start.3
  7.2 0.0 copy-start.4
  7.2 0.0 all-gather.3.cloned.1.call-start
  7.2 0.7 all-gather.3.cloned.1.call-update
  7.9 0.0 copy-start.6
  7.9 0.0 all-gather.5.cloned.1.call-start
  8.0 0.7 all-gather.5.cloned.1.call-update
  8.7 0.0 copy-done.3
  8.7 0.0 copy-done
  8.7 0.0 copy-done.4
  8.8 0.5 fusion.2
  9.2 0.1 mul.53
  9.3 2.3 bitcast_multiply_fusion
  11.6 287.3 %all-gather.3.cloned.1.call-done = bf16[4096,7168]{1,0:T(8,128)(2,1)} async-done(((bf16[256,7168]{1,0:T(8,128)(2,1)}), bf16[4096,7168]{1,0:T(8,128)(2,1)}) %all-gather.3.cloned.1.call-update) | async-done | bytes 58720272 | tf_op jit(solution)/shard_map/all_gather | solution.py:28
  298.9 0.0 copy-done.6
  298.9 23.6 %multiply_reduce_fusion = (f32[128]{0:T(128)S(1)}, bf16[128,7168]{1,0:T(8,128)(2,1)}) fusion(bf16[128,7168]{1,0:T(8,128)(2,1)S(1)} %copy-done.6, f32[128,7168]{1,0:T(8,128)} %bitcast_multiply_fusion, bf16[128,4096]{1,0:T(8,128)(2,1)S(1)} %copy-done, bf16[4096,7168]{1,0:T(8,128)(2,1)} %all-gather.3.cloned.1.call-done), kind=kOutput, calls=%fused_computation.4 | convolution fusion | flops 7524450304 | bytes 67109376 | tf_op jit(solution)/shard_map/dot_general | solution.py:26
  322.5 0.1 reduce_sum.35
  322.6 0.1 reduce_sum.36
  322.7 4.9 %psum.21 = f32[8]{0:T(128)S(1)} all-reduce(f32[8]{0:T(128)S(1)} %reduce_sum.36), channel_id=1, replica_groups=mesh['pop'=16,'shard'=2] {'shard'}, use_global_device_ids=true, to_apply=%region_2.3 | all-reduce | flops 8 | bytes 64 | tf_op jit(solution)/shard_map/psum | solution.py:43
  327.7 0.6 fusion.5
  328.3 32.1 %all-reduce = (f32[]{:T(128)}, f32[]{:T(128)}) all-reduce(f32[]{:T(128)} %get-tuple-element.4, f32[]{:T(128)} %get-tuple-element.3), channel_id=1, replica_groups=mesh['pop'=16,'shard'=2] {'pop'}, use_global_device_ids=true, to_apply=%region_6.7 | all-reduce | flops 2 | bytes 16 | tf_op jit(solution)/shard_map/psum | solution.py:44
  363.0 0.0 copy-start.5
  363.0 0.1 convert_multiply_fusion
  363.1 10.5 %all_to_all.19 = f32[8,16,256]{2,0,1:T(8,128)S(1)} all-to-all(f32[8,16,256]{2,0,1:T(8,128)S(1)} %bitcast.22), channel_id=1, replica_groups=mesh['pop'=16,'shard'=2] {'pop'}, dimensions={1} | all-to-all | bytes 262144 | tf_op jit(solution)/shard_map/all_to_all | solution.py:49
  373.6 0.0 all-gather.5.cloned.1.call-done
  373.7 0.0 copy-start.2
  373.7 2.8 fusion.6
  376.4 0.0 copy-done.5
  376.5 0.0 copy-done.2
  376.5 0.0 copy-start.1
  376.5 4.2 %fusion = f32[256,7168]{1,0:T(8,128)} fusion(f32[256,7168]{1,0:T(8,128)S(1)} %fusion.6, bf16[128,7168]{1,0:T(8,128)(2,1)S(1)} %copy-done.2, f32[8,16,256]{2,0,1:T(8,128)S(1)} %all_to_all.19, bf16[128,256]{1,0:T(8,128)(2,1)S(1)} %bitcast_convert_fusion), kind=kOutput, calls=%fused_computation.1 | convolution fusion | flops 473530368 | bytes 16711680 | tf_op jit(solution)/shard_map/dot_general | solution.py:54
  380.7 0.0 copy-done.1
  (4 shorter events, 0.0 us)
Async XLA Ops:
  7.2 1.6 copy-start
  7.2 1.5 copy-start.3
  7.2 1.6 copy-start.4
  7.2 291.7 %all-gather.3.cloned.1.call-start = ((), (), s32[]{:S(2)}) async-start(), calls=%async_computation.1 | async-start | bytes 62390272 | tf_op jit(solution)/shard_map/all_gather | solution.py:28
  7.9 291.0 %copy-start.6 = (bf16[128,7168]{1,0:T(8,128)(2,1)S(1)}, bf16[128,7168]{1,0:T(8,128)(2,1)}, u32[]{:S(2)}) copy-start(bf16[128,7168]{1,0:T(8,128)(2,1)} %param.9) | copy-start | bytes 5505028
  7.9 365.7 %all-gather.5.cloned.1.call-start = ((), (), s32[]{:S(2)}) async-start(), calls=%async_computation.2 | async-start | bytes 1949696 | tf_op jit(solution)/shard_map/all_gather | solution.py:52
  363.0 13.4 %copy-start.5 = (f32[8]{0:T(128)}, f32[8]{0:T(128)S(1)}, u32[]{:S(2)}) copy-start(f32[8]{0:T(128)S(1)} %subtract_divide_fusion) | copy-start | bytes 100
  373.7 2.8 copy-start.2
  376.5 4.2 %copy-start.1 = (bf16[128,4096]{1,0:T(8,128)(2,1)S(1)}, bf16[128,4096]{1,0:T(8,128)(2,1)}, u32[]{:S(2)}) copy-start(bf16[128,4096]{1,0:T(8,128)(2,1)} %param.5) | copy-start | bytes 3145732
Sparse Core Ops, SparseCore 0:
  9.6 289.2 all-gather.2
  301.2 40.6 all-gather.4
where the time goes:
time: 388 us
  waiting for transfers between devices  289 us (74%)
  blocking collectives  47.5 us (12%)
  matrix products  31 us (8%)
  between operations  16.8 us (4%)
    all_gather x1, waiting for transfers between devices, local(): lax.all_gather(weight, 'pop', axis=0, tiled=True)  287 us
    psum x1, blocking collectives, local(): lax.psum((jnp.sum(reward), jnp.sum(reward * reward)), 'pop')  32.1 us
    dot_general x1, matrix products, local(): jnp.dot(hidden, lax.all_gather(weight, 'pop', axis=0, tiled=True), prefer...  23.6 us
    all_to_all x1, blocking collectives, local(): lax.all_to_all(weighted, 'pop', split_axis=1, concat_axis=0, tiled=True)  10.5 us
  transfers between devices with their start and end apart: 2, of which 1 were waited for; matrix products, arithmetic and copies ran while one was open for 7% of the time, Pallas kernels for 0%

commit v1 on v0

v1 whole, which is shorter than its diff:
```python
import functools
import math

import jax
import jax.numpy as jnp
from jax import lax
from jax.experimental import pallas as pl
from jax.experimental.pallas import tpu as pltpu
from jax.sharding import PartitionSpec as P

noise_scale = 0.5
spread_eps = 1e-05
lane = 128


def group_size(pop, cols):
    size = 1
    while size * 2 <= min(pop, 8) and cols % (size * 2 * lane) == 0:
        size *= 2
    return size


def high_bits(size):
    bits = []
    bit = size // 2
    while bit:
        bits.append(bit)
        bit //= 2
    return bits


def spans(bits):
    held = [0]
    out = []
    for bit in bits:
        out.append((bit, list(held)))
        held = held + [m ^ bit for m in held]
    return out


def greet(me, shard, pop_masks, shard_masks):
    barrier = pltpu.get_barrier_semaphore()
    for mask in pop_masks:
        pl.semaphore_signal(barrier, inc=1, device_id={"pop": me ^ mask},
                            device_id_type=pl.DeviceIdType.MESH)
    for mask in shard_masks:
        pl.semaphore_signal(barrier, inc=1, device_id={"shard": shard ^ mask},
                            device_id_type=pl.DeviceIdType.MESH)
    pl.semaphore_wait(barrier, len(pop_masks) + len(shard_masks))


def gather_kernel(pop, shards, group, counts,
                  hidden, weight, left, right, target,
                  hidden_all, weight_all, left_all, right_all, target_all,
                  h_send, h_recv, w_send, w_recv, l_send, l_recv,
                  r_send, r_recv, t_send, t_recv, own_sem):
    me = lax.axis_index("pop")
    shard = lax.axis_index("shard")
    rank = lax.rem(me, group)
    rows = hidden.shape[0]
    piece = rows // shards
    cols = weight.shape[1] // group

    def remote(src, dst, send, recv, **where):
        copy = pltpu.make_async_remote_copy(
            src_ref=src, dst_ref=dst, send_sem=send, recv_sem=recv,
            device_id=where, device_id_type=pl.DeviceIdType.MESH)
        copy.start()
        return copy

    def block_of(r):
        return pl.ds(pl.multiple_of(r * cols, lane), cols)

    started = []
    own = [
        (hidden, hidden_all.at[rank]),
        (weight.at[:, block_of(rank)], weight_all.at[me]),
        (left, left_all.at[me]),
        (right, right_all.at[me]),
        (target.at[:, block_of(rank)], target_all.at[rank]),
    ]

    greet(me, shard, list(range(1, pop)), list(range(1, shards)))

    part = pl.ds(pl.multiple_of(shard * piece, piece), piece)
    group_bits = high_bits(group)
    outer_bits = [b for b in group_bits if b > 1]
    inner_bits = [b for b in group_bits if b == 1]

    weight_order = sorted(range(1, pop), key=lambda k: -(k >> 1))
    weight_queue = list(weight_order)

    def push_weight(n):
        for _ in range(n):
            if not weight_queue:
                return
            k = weight_queue.pop(0)
            other = me ^ k
            started.append(remote(
                weight.at[:, block_of(lax.rem(other, group))], weight_all.at[me],
                w_send.at[k - 1], w_recv.at[k - 1], pop=other))

    hid = [0]

    def hidden_copy(mask, rows_of, **where):
        i = hid[0]
        hid[0] += 1
        r = rank ^ mask
        src = hidden if mask == 0 else hidden_all.at[r]
        dst = hidden_all.at[r]
        if rows_of is not None:
            src, dst = src.at[rows_of], dst.at[rows_of]
        return remote(src, dst, h_send.at[i], h_recv.at[i], **where)

    fac = [0]

    def factor_copies(bit, held):
        out = []
        for mask in held:
            i = fac[0]
            fac[0] += 1
            r = me ^ mask
            out.append(remote(left if mask == 0 else left_all.at[r], left_all.at[r],
                              l_send.at[i], l_recv.at[i], pop=me ^ bit))
            out.append(remote(right if mask == 0 else right_all.at[r], right_all.at[r],
                              r_send.at[i], r_recv.at[i], pop=me ^ bit))
        return out

    outer = spans(outer_bits)
    factor_steps = spans(high_bits(pop))
    held_all = [0]
    for bit in outer_bits:
        held_all = held_all + [m ^ bit for m in held_all]

    wait_factor = []
    local = []
    for i in range(max(len(outer), 1)):
        mine = []
        if i < len(outer):
            bit, held = outer[i]
            for mask in held:
                mine.append(hidden_copy(mask, part, pop=me ^ bit))
        for c in wait_factor:
            c.wait_recv()
        if i < len(factor_steps):
            wait_factor = factor_copies(*factor_steps[i])
            started.extend(wait_factor)
        push_weight(4)
        if i == 0:
            for j, (src, dst) in enumerate(own):
                copy = pltpu.make_async_copy(src, dst, own_sem.at[j])
                copy.start()
                local.append(copy)
            for k in range(1, group):
                started.append(remote(
                    target.at[:, block_of(rank ^ k)], target_all.at[rank],
                    t_send.at[k - 1], t_recv.at[k - 1], pop=me ^ k))
        for c in mine:
            c.wait_recv()
        started.extend(mine)
    cross = []
    for j in range(1, shards):
        for mask in held_all[1:]:
            cross.append(hidden_copy(mask, part, shard=shard ^ j))
    for step in factor_steps[max(len(outer), 1):]:
        for c in wait_factor:
            c.wait_recv()
        wait_factor = factor_copies(*step)
        started.extend(wait_factor)
        push_weight(3)
    push_weight(len(weight_queue))
    for c in cross:
        c.wait_recv()
    started.extend(cross)
    last = []
    for bit in inner_bits:
        for mask in held_all:
            last.append(hidden_copy(mask, None, pop=me ^ bit))
    for c in last + wait_factor:
        c.wait_recv()
    started.extend(last)
    for c in started:
        c.wait_send()
    for k in range(1, pop):
        pltpu.make_async_remote_copy(
            src_ref=weight.at[:, block_of(rank)], dst_ref=weight_all.at[me ^ k],
            send_sem=w_send.at[k - 1], recv_sem=w_recv.at[k - 1],
            device_id={"pop": me ^ k}, device_id_type=pl.DeviceIdType.MESH).wait_recv()
    for k in range(1, group):
        pltpu.make_async_remote_copy(
            src_ref=target.at[:, block_of(rank)], dst_ref=target_all.at[rank ^ k],
            send_sem=t_send.at[k - 1], recv_sem=t_recv.at[k - 1],
            device_id={"pop": me ^ k}, device_id_type=pl.DeviceIdType.MESH).wait_recv()
    for c in local:
        c.wait()


def return_kernel(group, blocks, out, send, recv, own_sem):
    me = lax.axis_index("pop")
    rank = lax.rem(me, group)
    cols = blocks.shape[2]
    place = pl.ds(pl.multiple_of(rank * cols, lane), cols)
    local = pltpu.make_async_copy(blocks.at[rank], out.at[:, place], own_sem)
    local.start()
    greet(me, 0, list(range(1, group)), [])
    copies = []
    for k in reversed(range(1, group)):
        copy = pltpu.make_async_remote_copy(
            src_ref=blocks.at[rank ^ k], dst_ref=out.at[:, place],
            send_sem=send.at[k - 1], recv_sem=recv.at[k - 1],
            device_id={"pop": me ^ k}, device_id_type=pl.DeviceIdType.MESH)
        copy.start()
        copies.append(copy)
    for copy in copies:
        copy.wait()
    local.wait()


def split_parts(values):
    high = values.astype(jnp.bfloat16)
    kept = lax.optimization_barrier(high)
    low = (values - kept.astype(jnp.float32)).astype(jnp.bfloat16)
    return (high, low)


def local(hidden, weight, left_factors, right_factors, target):
    pop = lax.axis_size("pop")
    shards = lax.axis_size("shard")
    members, features = left_factors.shape
    rows = hidden.shape[0]
    tokens = rows // members
    depth, local_cols = weight.shape
    group = group_size(pop, local_cols)
    cols = local_cols // group
    member_count = members * pop
    me = lax.axis_index("pop")
    base = (me // group) * group

    anyspace = pl.BlockSpec(memory_space=pl.ANY)
    dma = pltpu.SemaphoreType.DMA
    half = max(group // 2, 1)
    hcount = (half - 1) + (half - 1) * (shards - 1) + (half if group > 1 else 0)
    hcount = max(hcount, 1)
    tcount = max(group - 1, 1)
    fcount = max(pop - 1, 1)
    bf16 = jnp.bfloat16
    hidden_all, weight_all, left_all, right_all, target_all = pl.pallas_call(
        functools.partial(gather_kernel, pop, shards, group, None),
        out_shape=(
            jax.ShapeDtypeStruct((group, rows, features), bf16),
            jax.ShapeDtypeStruct((pop, depth, cols), bf16),
            jax.ShapeDtypeStruct((pop, members, features), bf16),
            jax.ShapeDtypeStruct((pop, members, local_cols), bf16),
            jax.ShapeDtypeStruct((group, rows, cols), bf16),
        ),
        in_specs=[anyspace] * 5,
        out_specs=[anyspace] * 5,
        scratch_shapes=[
            dma((hcount,)), dma((hcount,)), dma((fcount,)), dma((fcount,)),
            dma((fcount,)), dma((fcount,)), dma((fcount,)), dma((fcount,)),
            dma((tcount,)), dma((tcount,)), dma((5,)),
        ],
        compiler_params=pltpu.CompilerParams(collective_id=0, has_side_effects=True),
    )(hidden, weight, left_factors, right_factors, target)

    group_members = group * members
    base_out = jnp.dot(
        hidden_all.reshape(group * rows, features),
        weight_all.reshape(pop * depth, cols),
        preferred_element_type=jnp.float32,
    )
    left_group = lax.dynamic_slice_in_dim(left_all, base, group, 0)
    right_group = lax.dynamic_slice(
        right_all, (base, 0, (me % group) * cols), (group, members, cols)
    ).reshape(group_members, cols)
    projected = jnp.einsum(
        "mtd,md->mt",
        hidden_all.reshape(group_members, tokens, features),
        left_group.reshape(group_members, features),
        preferred_element_type=jnp.float32,
    ) / math.sqrt(features)
    perturbed = (
        base_out.reshape(group_members, tokens, cols)
        + noise_scale * projected[:, :, None] * right_group.astype(jnp.float32)[:, None, :]
    )
    blocks = perturbed.astype(bf16).reshape(group, rows, cols)
    directions = target_all.reshape(group_members, tokens, cols).astype(jnp.float32)
    partial_value = jnp.sum(jax.nn.silu(perturbed) * directions, axis=(1, 2))
    placed = lax.dynamic_update_slice_in_dim(
        jnp.zeros((member_count,), jnp.float32), partial_value, base * members, 0)
    reward = lax.psum(placed, ("pop", "shard"))

    up_out = pl.pallas_call(
        functools.partial(return_kernel, group),
        out_shape=jax.ShapeDtypeStruct((rows, local_cols), bf16),
        in_specs=[anyspace],
        out_specs=anyspace,
        scratch_shapes=[dma((tcount,)), dma((tcount,)), dma(())],
        compiler_params=pltpu.CompilerParams(collective_id=1, has_side_effects=True),
    )(blocks)

    centered = reward - jnp.sum(reward) / member_count
    spread = jnp.sum(centered * centered) / member_count
    fitness_all = centered / jnp.sqrt(spread + spread_eps)
    fitness = lax.dynamic_slice_in_dim(fitness_all, me * members, members, 0)
    left_mine = lax.dynamic_slice_in_dim(
        left_all.reshape(member_count, features), me * depth, depth, 1)
    weighted = left_mine.astype(jnp.float32) * fitness_all[:, None]
    high, low = split_parts(weighted)
    contract = (((0,), (0,)), ((), ()))
    portion = right_all.reshape(member_count, local_cols)
    upper = lax.dot_general(high, portion, contract, preferred_element_type=jnp.float32)
    lower = lax.dot_general(low, portion, contract, preferred_element_type=jnp.float32)
    step = (upper + lower) / math.sqrt(member_count)
    return (up_out, step, fitness)


def solution(mesh):
    in_specs = (
        P("pop", None),
        P("pop", "shard"),
        P("pop", None),
        P("pop", "shard"),
        P("pop", "shard"),
    )
    out_specs = (P("pop", "shard"), P("pop", "shard"), P("pop"))
    return jax.shard_map(local, mesh=mesh, in_specs=in_specs, out_specs=out_specs, check_vma=False)
```

time: 388 us -> 281 us (0.72)
  waiting for transfers between devices: 289 us -> 0 us
  Pallas kernels: 0 us -> 204 us
  between operations: 16.8 us -> 2.07 us
  blocking collectives: 47.5 us -> 39.8 us
  local copies, waits for them, and re-layouts: 0.21 us -> 4.74 us
    all_gather x2 -> x0, waiting for transfers between devices: 287 us -> none  [the longest x1 287 us: local(): lax.all_gather(weight, 'pop', axis=0, tiled=True)]
    pallas_call x0 -> x2, Pallas kernels: none -> 204 us  [the longest x1 179 us: local(): pl.pallas_call(functools.partial(gather_kernel, pop, shards, group, None)...]
    all_to_all x1 -> x0, blocking collectives: 10.5 us -> none  [local(): lax.all_to_all(weighted, 'pop', split_axis=1, concat_axis=0, tiled=True)]
    psum x2 -> x1, blocking collectives: 37 us -> 39.8 us  [local(): reward = lax.psum(placed, ('pop', 'shard'))]
  transfers between devices with their start and end apart: 2 -> 0, of which waited for: 1 -> 0; matrix products, arithmetic and copies ran while one was open for 7% -> 0% of each run, Pallas kernels for 0% -> 0%
where the time goes in v1:
time: 281 us
  Pallas kernels  204 us (73%)
  blocking collectives  39.8 us (14%)
  matrix products  28.4 us (10%)
  local copies, waits for them, and re-layouts  4.74 us (2%)
    pallas_call x1, Pallas kernels, local(): pl.pallas_call(functools.partial(gather_kernel, pop, shards, group, None)...  179 us
    psum x1, blocking collectives, local(): reward = lax.psum(placed, ('pop', 'shard'))  39.8 us
    pallas_call x1, Pallas kernels, local(): pl.pallas_call(functools.partial(return_kernel, group), out_shape=jax.Sha...  25.2 us
    dot_general x1, matrix products, local(): jnp.dot(hidden_all.reshape(group * rows, features), weight_all.reshape(po...  15.5 us
    dot_general x1, matrix products, local(): jnp.einsum('mtd,md->mt', hidden_all.reshape(group_members, tokens, featur...  6.66 us

profile of v1, /device:TPU:0, one launch (start us, length us, event | category | flops | bytes accessed | tf_op | source)
XLA Modules:
  0.0 280.9 jit_solution(3675065162624216967)
XLA Ops:
  0.7 178.5 %shard_map.76 = (bf16[8,128,4096]{2,1,0:T(8,128)(2,1)}, bf16[16,256,896]{2,1,0:T(8,128)(2,1)}, bf16[16,8,4096]{2,1,0:T(8,128)(2,1)}, bf16[16,8,7168]{2,1,0:T(8,128)(2,1)}, bf16[8,128,896]{2,1,0:T(8,128)(2,1)}) custom-call(bf16[128,4096]{1,0:T(8,128)(2,1)} %hidden.1, bf16[256,7168]{1,0:T(8,128)(2,1)} %weight.1, bf16[8,4096]{1,0:T(8,128)(2,1)} %left.1, ...), custom_call_target="tpu_custom_call" | custom-call | tf_op jit(solution)/shard_map/pallas_call | solution.py:247
  179.2 1.1 dynamic-slice_bitcast_fusion
  180.3 0.0 copy-start
  180.3 6.7 %fusion.6 = f32[64,1,16]{2,1,0:T(1,128)S(1)} fusion(bf16[64,16,4096]{2,1,0:T(8,128)(2,1)} %bitcast.30, bf16[64,4096,1]{1,0,2:T(8,128)(2,1)S(1)} %dynamic-slice_bitcast_fusion), kind=kOutput, calls=%fused_computation.9 | convolution fusion | flops 8388608 | bytes 8916992 | tf_op jit(solution)/shard_map/mtd,md->mt/dot_general | solution.py:276
  186.9 0.0 copy-done
  187.0 15.5 %fusion.1 = (f32[64]{0:T(128)S(1)}, bf16[64,16,896]{2,1,0:T(8,128)(2,1)}) fusion(bf16[64,16,896]{2,1,0:T(8,128)(2,1)} %bitcast.33, f32[64,896]{1,0:T(8,128)S(1)} %bitcast_convert_fusion, f32[64,16]{1,0:T(8,128)S(1)} %broadcast_multiply_fusion, bf16[64,16,4096]{2,1,0:T(8,128)(2,1)} %bitcast.31, bf16[4096,896,1]{1,0,2:T(8,128)(2,1)} %bitcast.32), kind=kOutput, calls=%fused_computation.3 | convolution fusion | flops 7525367808 | bytes 19632384 | tf_op jit(solution)/shard_map/dot_general | solution.py:267
  202.5 0.2 dynamic_update_slice.3
  202.7 39.8 %psum.7 = f32[128]{0:T(128)S(1)} all-reduce(f32[128]{0:T(128)S(1)} %dynamic_update_slice.3), channel_id=1, replica_groups=mesh['pop'=16,'shard'=2] {'pop','shard'}, use_global_device_ids=true, to_apply=%region_1.2 | all-reduce | flops 128 | bytes 1024 | tf_op jit(solution)/shard_map/psum | solution.py:291
  242.5 0.6 reduce_sum.28
  243.8 0.6 multiply_reduce_fusion
  245.1 0.9 fusion.8
  246.0 1.1 fusion.4
  247.2 5.1 %fusion = f32[256,7168]{1,0:T(8,128)} fusion(f32[256,7168]{1,0:T(8,128)S(1)} %fusion.4, bf16[16,8,7168]{2,1,0:T(8,128)(2,1)S(1)} %copy-done, bf16[128,256]{1,0:T(8,128)(2,1)S(1)} %fusion.8, f32[128]{0:T(128)S(1)} %subtract_divide_fusion, bf16[128,4096]{1,0:T(8,128)(2,1)} %bitcast.28, s32[]{:T(128)S(6)} %select_n.31), kind=kOutput, calls=%fused_computation.1 | convolution fusion | flops 473595904 | bytes 16646660 | tf_op jit(solution)/shard_map/dot_general | solution.py:313
  252.3 0.6 dynamic_slice.15
  252.8 25.2 %shard_map.77 = bf16[128,7168]{1,0:T(8,128)(2,1)} custom-call(bf16[8,128,896]{2,1,0:T(8,128)(2,1)} %bitcast.26), custom_call_target="tpu_custom_call" | custom-call | tf_op jit(solution)/shard_map/pallas_call | solution.py:293
  278.1 2.8 %copy.14 = bf16[128,7168]{1,0:T(8,128)(2,1)} copy(bf16[128,7168]{1,0:T(8,128)(2,1)} %shard_map.77) | data formatting | bytes 3670016
  (4 shorter events, 0.0 us)
Async XLA Ops:
  180.3 6.7 %copy-start = (bf16[16,8,7168]{2,1,0:T(8,128)(2,1)S(1)}, bf16[16,8,7168]{2,1,0:T(8,128)(2,1)}, u32[]{:S(2)}) copy-start(bf16[16,8,7168]{2,1,0:T(8,128)(2,1)} %get-tuple-element.11) | copy-start | bytes 5505028

commit v2 on v0

v2 whole, which is shorter than its diff:
```python
import functools
import math

import jax
import jax.numpy as jnp
from jax import lax
from jax.experimental import pallas as pl
from jax.experimental.pallas import tpu as pltpu
from jax.sharding import PartitionSpec as P

noise_scale = 0.5
spread_eps = 1e-05
lane = 128


def group_size(pop, cols):
    size = 1
    while size * 2 <= min(pop, 8) and cols % (size * 2 * lane) == 0:
        size *= 2
    return size


def high_bits(size):
    bits = []
    bit = size // 2
    while bit:
        bits.append(bit)
        bit //= 2
    return bits


def spans(bits):
    held = [0]
    out = []
    for bit in bits:
        out.append((bit, list(held)))
        held = held + [m ^ bit for m in held]
    return out


def greet(me, shard, pop_masks, shard_masks):
    barrier = pltpu.get_barrier_semaphore()
    for mask in pop_masks:
        pl.semaphore_signal(barrier, inc=1, device_id={"pop": me ^ mask},
                            device_id_type=pl.DeviceIdType.MESH)
    for mask in shard_masks:
        pl.semaphore_signal(barrier, inc=1, device_id={"shard": shard ^ mask},
                            device_id_type=pl.DeviceIdType.MESH)
    pl.semaphore_wait(barrier, len(pop_masks) + len(shard_masks))


def chunks_of(cols):
    out = []
    start = 0
    while start < cols:
        width = min(2 * lane, cols - start)
        out.append((start, width))
        start += width
    return out


def fused_kernel(pop, shards, group, tokens,
                 hidden, weight, left, right, target,
                 up_out, left_all, right_all, rewards,
                 hidden_v, weight_v, target_v, up_v, left_v, right_v, proj_v, racc, rsum, rmine, rall,
                 h_send, h_recv, w_send, w_recv, l_send, l_recv,
                 r_send, r_recv, t_send, t_recv, u_send, u_recv,
                 s_send, s_recv, p_send, p_recv, own_sem, own_up, pre_sem):
    me = lax.axis_index("pop")
    shard = lax.axis_index("shard")
    rank = lax.rem(me, group)
    base = me - rank
    rows, features = hidden.shape
    members = left.shape[0]
    depth = weight.shape[0]
    piece = rows // shards
    cols = weight.shape[1] // group
    chunks = chunks_of(cols)

    def remote(src, dst, send, recv, **where):
        return pltpu.make_async_remote_copy(
            src_ref=src, dst_ref=dst, send_sem=send, recv_sem=recv,
            device_id=where, device_id_type=pl.DeviceIdType.MESH)

    def columns(r, start, width):
        return pl.ds(pl.multiple_of(r * cols + start, lane), width)

    def row_block(r, size=rows):
        return pl.ds(pl.multiple_of(r * size, size), size)

    started = []

    def go(copy):
        copy.start()
        started.append(copy)
        return copy

    greet(me, shard, list(range(1, pop)), list(range(1, shards)))

    local = [
        pltpu.make_async_copy(hidden, hidden_v.at[row_block(rank), :], own_sem.at[0]),
        pltpu.make_async_copy(weight.at[:, columns(rank, 0, cols)],
                              weight_v.at[row_block(me, depth), :], own_sem.at[1]),
        pltpu.make_async_copy(left, left_all.at[me], own_sem.at[2]),
        pltpu.make_async_copy(right, right_all.at[me], own_sem.at[3]),
        pltpu.make_async_copy(target.at[:, columns(rank, 0, cols)],
                              target_v.at[row_block(rank), :], own_sem.at[4]),
    ]

    group_bits = high_bits(group)
    outer = spans([b for b in group_bits if b > 1])
    held_all = [0]
    for bit, _ in outer:
        held_all = held_all + [m ^ bit for m in held_all]
    factor_steps = spans(high_bits(pop))
    order = sorted(range(1, pop), key=lambda k: -(k >> 1))

    def weight_copy(c, k, sender):
        start, width = chunks[c]
        there = pl.ds(start, width)
        return remote(
            weight.at[:, columns(lax.rem(me ^ k, group), start, width)],
            weight_v.at[row_block(sender, depth), there],
            w_send.at[c * (pop - 1) + k - 1], w_recv.at[c * (pop - 1) + k - 1], pop=me ^ k)

    def push_weights(c):
        if c < len(chunks):
            for k in order:
                go(weight_copy(c, k, me))

    def target_copy(k, sender_rank):
        return remote(
            target.at[:, columns(rank ^ k, 0, cols)], target_v.at[row_block(sender_rank), :],
            t_send.at[k - 1], t_recv.at[k - 1], pop=me ^ k)

    counts = [0, 0]

    def hidden_copy(mask, full, **where):
        i = counts[0]
        counts[0] += 1
        r = rank ^ mask
        size, first = (rows, 0) if full else (piece, shard * piece)
        src = (hidden.at[pl.ds(pl.multiple_of(first, size), size), :] if mask == 0 else
               hidden_v.at[pl.ds(pl.multiple_of(r * rows + first, size), size), :])
        dst = hidden_v.at[pl.ds(pl.multiple_of(r * rows + first, size), size), :]
        return go(remote(src, dst, h_send.at[i], h_recv.at[i], **where))

    def factor_copies(bit, held):
        out = []
        for mask in held:
            i = counts[1]
            counts[1] += 1
            r = me ^ mask
            out.append(go(remote(left if mask == 0 else left_all.at[r], left_all.at[r],
                                 l_send.at[i], l_recv.at[i], pop=me ^ bit)))
            out.append(go(remote(right if mask == 0 else right_all.at[r], right_all.at[r],
                                 r_send.at[i], r_recv.at[i], pop=me ^ bit)))
        return out

    def arrived(copies):
        for c in copies:
            c.wait_recv()

    pushed = 0
    waiting = []
    for i, (bit, held) in enumerate(outer):
        mine = [hidden_copy(mask, False, pop=me ^ bit) for mask in held]
        arrived(waiting)
        waiting = factor_copies(*factor_steps[i])
        push_weights(pushed)
        pushed += 1
        if i == 0:
            for copy in local:
                copy.start()
            for k in range(1, group):
                go(target_copy(k, rank))
        arrived(mine)
    cross = [hidden_copy(mask, False, shard=shard ^ j)
             for j in range(1, shards) for mask in held_all[1:]]
    if not outer:
        for copy in local:
            copy.start()
        for k in range(1, group):
            go(target_copy(k, rank))
    for step in factor_steps[len(outer):]:
        arrived(waiting)
        waiting = factor_copies(*step)
        push_weights(pushed)
        pushed += 1
    while pushed < len(chunks):
        push_weights(pushed)
        pushed += 1
    arrived(cross)
    last = [hidden_copy(mask, True, pop=me ^ 1) for mask in held_all]
    arrived(waiting)
    for copy in local:
        copy.wait()
    near = [
        pltpu.make_async_copy(left_all.at[pl.ds(base, group)], left_v, pre_sem.at[0]),
        pltpu.make_async_copy(right_all.at[pl.ds(base, group), :, columns(rank, 0, cols)],
                              right_v, pre_sem.at[1]),
    ]
    for copy in near:
        copy.start()
    for copy in near:
        copy.wait()
    arrived(last)
    for k in range(1, group):
        target_copy(k, rank ^ k).wait_recv()

    half = group * rows // 2
    half_members = half // tokens
    total_members = group * members
    left_rows = left_v[...].astype(jnp.float32).reshape(total_members, features).astype(jnp.bfloat16)

    def project(h, carry):
        at = pl.ds(pl.multiple_of(h * half, half), half)
        full = lax.dot_general(hidden_v[at, :], left_rows, (((1,), (1,)), ((), ())),
                               preferred_element_type=jnp.float32)
        row = lax.broadcasted_iota(jnp.int32, full.shape, 0) + h * half
        member = lax.broadcasted_iota(jnp.int32, full.shape, 1)
        first = member * tokens
        keep = (row >= first) & (row < first + tokens)
        proj_v[at, :] = (noise_scale / math.sqrt(features)) * jnp.sum(
            jnp.where(keep, full, 0.0), axis=1, keepdims=True)
        return carry

    lax.fori_loop(0, 2, project, 0)
    racc[...] = jnp.zeros_like(racc)

    for c, (start, width) in enumerate(chunks):
        for k in order:
            weight_copy(c, k, me ^ k).wait_recv()
        span = pl.ds(start, width)

        def compute(h, carry, span=span, width=width):
            at = pl.ds(pl.multiple_of(h * half, half), half)
            base_out = jnp.dot(hidden_v[at, :], weight_v[:, span],
                               preferred_element_type=jnp.float32)
            wide = right_v[pl.ds(h * (group // 2), group // 2), :, span].astype(jnp.float32)
            wide = wide.reshape(half_members, width)
            wide = jnp.broadcast_to(wide[:, None, :], (half_members, tokens, width))
            perturbed = base_out + proj_v[at, :] * wide.reshape(half, width)
            up_v[at, span] = perturbed.astype(jnp.bfloat16)
            term = perturbed / (1.0 + jnp.exp(-perturbed)) * target_v[at, span].astype(jnp.float32)
            summed = jnp.sum(term.reshape(half_members, tokens, width), axis=1)
            line = summed[:, :lane]
            for j in range(1, width // lane):
                line = line + summed[:, j * lane:(j + 1) * lane]
            mine = pl.ds(pl.multiple_of(h * half_members, half_members), half_members)
            racc[mine, :] = racc[mine, :] + line
            return carry

        lax.fori_loop(0, 2, compute, 0)
        for k in reversed(range(1, group)):
            i = c * (group - 1) + k - 1
            go(remote(up_v.at[row_block(rank ^ k), span], up_out.at[:, columns(rank, start, width)],
                      u_send.at[i], u_recv.at[i], pop=me ^ k))
        copy = pltpu.make_async_copy(up_v.at[row_block(rank), span],
                                     up_out.at[:, columns(rank, start, width)], own_up.at[c])
        copy.start()
        local.append(copy)

    line = jnp.sum(jnp.transpose(racc[...]), axis=0, keepdims=True)
    rmine[...] = jnp.zeros_like(rmine)
    rmine[0:1, 0:total_members] = line[:, :total_members]
    ahead = [go(remote(rmine, rsum.at[j - 1], s_send.at[j - 1], s_recv.at[j - 1], shard=shard ^ j))
             for j in range(1, shards)]
    arrived(ahead)
    value = rmine[...]
    for j in range(1, shards):
        value = value + rsum[j - 1]
    rall[me] = value
    out = [go(remote(rall.at[me], rall.at[me], p_send.at[k - 1], p_recv.at[k - 1], pop=me ^ k))
           for k in range(1, pop)]
    for k in range(1, pop):
        remote(rall.at[me], rall.at[me ^ k], p_send.at[k - 1], p_recv.at[k - 1],
               pop=me ^ k).wait_recv()
    for c in range(len(chunks)):
        start, width = chunks[c]
        for k in range(1, group):
            i = c * (group - 1) + k - 1
            remote(up_v.at[row_block(rank ^ k), pl.ds(start, width)],
                   up_out.at[:, columns(rank ^ k, start, width)],
                   u_send.at[i], u_recv.at[i], pop=me ^ k).wait_recv()
    for copy in started:
        copy.wait_send()
    for copy in local[5:]:
        copy.wait()
    rewards[...] = rall[...]


def split_parts(values):
    high = values.astype(jnp.bfloat16)
    kept = lax.optimization_barrier(high)
    low = (values - kept.astype(jnp.float32)).astype(jnp.bfloat16)
    return (high, low)


def local(hidden, weight, left_factors, right_factors, target):
    pop = lax.axis_size("pop")
    shards = lax.axis_size("shard")
    members, features = left_factors.shape
    rows = hidden.shape[0]
    tokens = rows // members
    depth, local_cols = weight.shape
    group = group_size(pop, local_cols)
    cols = local_cols // group
    member_count = members * pop
    me = lax.axis_index("pop")

    anyspace = pl.BlockSpec(memory_space=pl.ANY)
    dma = pltpu.SemaphoreType.DMA
    half = group // 2
    hcount = (half - 1) * shards + half
    tcount = group - 1
    fcount = pop - 1
    nchunks = len(chunks_of(cols))
    bf16 = jnp.bfloat16
    group_rows = group * rows
    scratch = [
        pltpu.VMEM((group_rows, features), bf16),
        pltpu.VMEM((pop * depth, cols), bf16),
        pltpu.VMEM((group_rows, cols), bf16),
        pltpu.VMEM((group_rows, cols), bf16),
        pltpu.VMEM((group, members, features), bf16),
        pltpu.VMEM((group, members, cols), bf16),
        pltpu.VMEM((group_rows, 1), jnp.float32),
        pltpu.VMEM((group * members, lane), jnp.float32),
        pltpu.VMEM((max(shards - 1, 1), 8, lane), jnp.float32),
        pltpu.VMEM((8, lane), jnp.float32),
        pltpu.VMEM((pop, 8, lane), jnp.float32),
    ]
    for count in (hcount, nchunks * fcount, fcount, fcount, tcount, nchunks * tcount,
                  max(shards - 1, 1), fcount):
        scratch += [dma((count,)), dma((count,))]
    scratch += [dma((5,)), dma((nchunks,)), dma((2,))]
    up_out, left_all, right_all, rewards = pl.pallas_call(
        functools.partial(fused_kernel, pop, shards, group, tokens),
        out_shape=(
            jax.ShapeDtypeStruct((rows, local_cols), bf16),
            jax.ShapeDtypeStruct((pop, members, features), bf16),
            jax.ShapeDtypeStruct((pop, members, local_cols), bf16),
            jax.ShapeDtypeStruct((pop, 8, lane), jnp.float32),
        ),
        in_specs=[anyspace] * 5,
        out_specs=[anyspace] * 3 + [pl.BlockSpec(memory_space=pltpu.VMEM)],
        scratch_shapes=scratch,
        compiler_params=pltpu.CompilerParams(
            collective_id=0, has_side_effects=True, vmem_limit_bytes=60 * 1024 * 1024),
    )(hidden, weight, left_factors, right_factors, target)
    group_members = group * members
    reward = jnp.sum(
        rewards[:, 0, :group_members].reshape(pop // group, group, group_members), axis=1
    ).reshape(member_count)

    centered = reward - jnp.sum(reward) / member_count
    spread = jnp.sum(centered * centered) / member_count
    fitness_all = centered / jnp.sqrt(spread + spread_eps)
    fitness = lax.dynamic_slice_in_dim(fitness_all, me * members, members, 0)
    left_mine = lax.dynamic_slice_in_dim(
        left_all.reshape(member_count, features), me * depth, depth, 1)
    weighted = left_mine.astype(jnp.float32) * fitness_all[:, None]
    high, low = split_parts(weighted)
    contract = (((0,), (0,)), ((), ()))
    portion = right_all.reshape(member_count, local_cols)
    upper = lax.dot_general(high, portion, contract, preferred_element_type=jnp.float32)
    lower = lax.dot_general(low, portion, contract, preferred_element_type=jnp.float32)
    step = (upper + lower) / math.sqrt(member_count)
    return (up_out, step, fitness)


def solution(mesh):
    in_specs = (
        P("pop", None),
        P("pop", "shard"),
        P("pop", None),
        P("pop", "shard"),
        P("pop", "shard"),
    )
    out_specs = (P("pop", "shard"), P("pop", "shard"), P("pop"))
    return jax.shard_map(local, mesh=mesh, in_specs=in_specs, out_specs=out_specs, check_vma=False)
```

time: 388 us -> 212 us (0.55)
  waiting for transfers between devices: 289 us -> 0 us
  Pallas kernels: 0 us -> 197 us
  blocking collectives: 47.5 us -> 0 us
  matrix products: 31 us -> 8.01 us
  between operations: 16.8 us -> 2.04 us
    all_gather x2 -> x0, waiting for transfers between devices: 287 us -> none  [the longest x1 287 us: local(): lax.all_gather(weight, 'pop', axis=0, tiled=True)]
    pallas_call x0 -> x1, Pallas kernels: none -> 197 us  [local(): pl.pallas_call(functools.partial(fused_kernel, pop, shards, group, tokens...]
    psum x2 -> x0, blocking collectives: 37 us -> none  [the longest x1 32.1 us: local(): lax.psum((jnp.sum(reward), jnp.sum(reward * reward)), 'pop')]
    dot_general x4 -> x2, matrix products: 31 us -> 8.01 us  [the longest x1 5.24 us: local(): lax.dot_general(low, portion, contract, preferred_element_type=jnp.float32)]
    all_to_all x1 -> x0, blocking collectives: 10.5 us -> none  [local(): lax.all_to_all(weighted, 'pop', split_axis=1, concat_axis=0, tiled=True)]
  transfers between devices with their start and end apart: 2 -> 0, of which waited for: 1 -> 0; matrix products, arithmetic and copies ran while one was open for 7% -> 0% of each run, Pallas kernels for 0% -> 0%
where the time goes in v2:
time: 212 us
  Pallas kernels  197 us (93%)
  matrix products  8.01 us (4%)
  other arithmetic  3.02 us (1%)
    pallas_call x1, Pallas kernels, local(): pl.pallas_call(functools.partial(fused_kernel, pop, shards, group, tokens...  197 us
    dot_general x1, matrix products, local(): lax.dot_general(low, portion, contract, preferred_element_type=jnp.float32)  5.24 us

profile of v2, /device:TPU:0, one launch (start us, length us, event | category | flops | bytes accessed | tf_op | source)
XLA Modules:
  0.0 211.8 jit_solution(2224333283993878001)
XLA Ops:
  0.6 196.8 %shard_map.76 = (bf16[128,7168]{1,0:T(8,128)(2,1)}, bf16[16,8,4096]{2,1,0:T(8,128)(2,1)}, bf16[16,8,7168]{2,1,0:T(8,128)(2,1)}, f32[16,8,128]{2,1,0:T(8,128)}) custom-call(bf16[128,4096]{1,0:T(8,128)(2,1)} %hidden.1, bf16[256,7168]{1,0:T(8,128)(2,1)} %weight.1, bf16[8,4096]{1,0:T(8,128)(2,1)} %left.1, bf16[8,7168]{1,0:T(8,128)(2,1)} %right.1, ...), custom_call_target="tpu_custom_call" | custom-call | tf_op jit(solution)/shard_map/pallas_call | solution.py:338
  197.5 1.5 slice_reduce_fusion
  199.6 0.6 multiply_reduce_fusion
  200.9 0.1 div.29
  201.0 0.6 dynamic_slice.7
  201.6 0.9 fusion.4
  202.5 0.0 copy-start
  202.5 2.8 %fusion.2 = f32[256,7168]{1,0:T(8,128)S(1)} fusion(bf16[128,256]{1,0:T(8,128)(2,1)S(1)} %fusion.4, bf16[16,8,7168]{2,1,0:T(8,128)(2,1)} %get-tuple-element.10), kind=kOutput, calls=%fused_computation.3 | convolution fusion | flops 469762048 | bytes 9240576 | tf_op jit(solution)/shard_map/dot_general | solution.py:367
  205.3 0.0 copy-done
  205.3 0.0 copy-start.1
  205.3 5.2 %fusion = f32[256,7168]{1,0:T(8,128)} fusion(f32[256,7168]{1,0:T(8,128)S(1)} %fusion.2, bf16[16,8,7168]{2,1,0:T(8,128)(2,1)S(1)} %copy-done, bf16[128,256]{1,0:T(8,128)(2,1)S(1)} %fusion.4, f32[128]{0:T(128)S(1)} %div.29, bf16[128,4096]{1,0:T(8,128)(2,1)} %bitcast.12, s32[]{:T(128)S(6)} %select_n.6), kind=kOutput, calls=%fused_computation.1 | convolution fusion | flops 473595904 | bytes 16646660 | tf_op jit(solution)/shard_map/dot_general | solution.py:368
  210.6 0.0 copy-done.1
  210.6 1.2 copy.9
  (2 shorter events, 0.0 us)
Async XLA Ops:
  202.5 2.8 %copy-start = (bf16[16,8,7168]{2,1,0:T(8,128)(2,1)S(1)}, bf16[16,8,7168]{2,1,0:T(8,128)(2,1)}, u32[]{:S(2)}) copy-start(bf16[16,8,7168]{2,1,0:T(8,128)(2,1)} %get-tuple-element.10) | copy-start | bytes 5505028
  205.3 5.3 %copy-start.1 = (bf16[128,7168]{1,0:T(8,128)(2,1)S(1)}, bf16[128,7168]{1,0:T(8,128)(2,1)}, u32[]{:S(2)}) copy-start(bf16[128,7168]{1,0:T(8,128)(2,1)} %get-tuple-element.16) | copy-start | bytes 5505028
